TPU v7x, 32 devices: a whole 2x2x4 slice. The times are simulated.
32 devices in a mesh: ctx: 4 (over z), kvh: 4 (over y, x), conv: 2 (over core).
Axes of the slice: x: 2, y: 2, z: 4, core: 2. Of those that a mesh axis runs over, the one named last changes fastest.
Arguments:
- queries: bfloat16 [2, 512, 64, 128], P('conv', 'ctx', 'kvh'), may hold values from -6 to 6
- keys: bfloat16 [2, 4096, 8, 128], P('conv', 'ctx', 'kvh'), may hold values from -6 to 6
- values: bfloat16 [2, 4096, 8, 128], P('conv', 'ctx', 'kvh'), may hold values from -6 to 6
- lengths: int32 [2], P('conv'), may hold values from 64 to 3584
Outputs:
- attended: bfloat16 [2, 512, 64, 128], P('conv', 'ctx', 'kvh')
Inputs may be any that keep to these rules, and one draw needn't show every extreme that they name: The new turn's keys and values stand at cache positions lengths to lengths + 511; later positions hold unused entries.
All inputs are finite; a program needn't handle non-finite values.
Results may differ from a plain program's by a relative error of at most 0.005.
Values may be sent and summed in bfloat16 or wider, within the bound.
No kernel may reach another device: no remote copies, remote signals or barrier semaphores. Data moves between devices by JAX's collectives and lax.ppermute only.
A program may use at most 64 MiB of HBM per device.

v0:
```python
import jax
import jax.numpy as jnp
from jax import lax
from jax.sharding import PartitionSpec as P

mask_fill = -1e30


def shards(queries, keys, values, lengths):
    conv_dev, tok_dev, head_dev, head_dim = queries.shape
    ctx_dev = keys.shape[1]
    kv_dev = keys.shape[2]
    group_size = head_dev // kv_dev
    cycle_size = lax.axis_size("ctx")
    score_scale = 1.0 / head_dim**0.5
    key_position = lax.axis_index("ctx") * ctx_dev + jnp.arange(ctx_dev, dtype=jnp.int32)
    piece_rows = lax.all_gather(queries, "ctx", axis=1, tiled=True)
    row_count = piece_rows.shape[1]
    block_size = 64
    block_total = row_count // block_size
    blocks = jnp.moveaxis(
        piece_rows.reshape(conv_dev, block_total, block_size, head_dev, head_dim), 1, 0
    )

    def one_block(block_args):
        query_block, block_index = block_args
        query_block = query_block.reshape(conv_dev, block_size, kv_dev, group_size, head_dim)
        scores = (
            jnp.einsum("cbkgd,cskd->ckbgs", query_block, keys, preferred_element_type=jnp.float32)
            * score_scale
        )
        query_position = (
            lengths[:, None]
            + block_index * block_size
            + jnp.arange(block_size, dtype=jnp.int32)[None, :]
        )
        visible = key_position[None, None, None, None, :] <= query_position[:, None, :, None, None]
        masked = jnp.where(visible, scores, mask_fill)
        row_max = jnp.max(masked, axis=-1)
        weights = jnp.where(visible, jnp.exp(masked - row_max[..., None]), 0.0)
        exp_total = jnp.sum(weights, axis=-1)
        rounded = weights.astype(jnp.bfloat16)
        weighted = jnp.einsum(
            "ckbgs,cskd->ckbgd", rounded, values, preferred_element_type=jnp.float32
        )
        safe_total = jnp.maximum(exp_total, 1.0)
        partial_value = (weighted / safe_total[..., None]).astype(jnp.bfloat16)
        log_total = row_max + jnp.log(safe_total)
        partial_value = jnp.transpose(partial_value, (0, 2, 1, 3, 4)).reshape(
            conv_dev, block_size, head_dev, head_dim
        )
        log_total = jnp.transpose(log_total, (0, 2, 1, 3)).reshape(conv_dev, block_size, head_dev)
        return (partial_value, log_total)

    partial_value, log_total = lax.map(
        one_block, (blocks, jnp.arange(block_total, dtype=jnp.int32))
    )
    partial_value = jnp.moveaxis(partial_value, 0, 1).reshape(
        conv_dev, row_count, head_dev, head_dim
    )
    log_total = jnp.moveaxis(log_total, 0, 1).reshape(conv_dev, row_count, head_dev)
    partial_value, log_total = (partial_value, log_total)
    arrived = lax.all_to_all(
        partial_value.reshape(conv_dev, cycle_size, tok_dev, head_dev, head_dim),
        "ctx",
        split_axis=1,
        concat_axis=1,
        tiled=True,
    )
    arrived_totals = lax.all_to_all(
        log_total.reshape(conv_dev, cycle_size, tok_dev, head_dev),
        "ctx",
        split_axis=1,
        concat_axis=1,
        tiled=True,
    )
    top = jnp.max(arrived_totals, axis=1)
    share = jnp.exp(arrived_totals - top[:, None])
    numerator = jnp.sum(share[..., None] * arrived.astype(jnp.float32), axis=1)
    denominator = jnp.sum(share, axis=1)
    return (numerator / denominator[..., None]).astype(jnp.bfloat16)


def solution(mesh):
    in_specs = (
        P("conv", "ctx", "kvh", None),
        P("conv", "ctx", "kvh", None),
        P("conv", "ctx", "kvh", None),
        P("conv"),
    )
    out_specs = P("conv", "ctx", "kvh", None)
    return jax.shard_map(shards, mesh=mesh, in_specs=in_specs, out_specs=out_specs, check_vma=False)
```

profile of v0, /device:TPU:0, one launch (start us, length us, event | category | flops | bytes accessed | tf_op | source)
XLA Modules:
  0.0 183.0 jit_solution(16355917170916339926)
XLA Ops:
  6.5 0.7 all-gather.2.cloned.1.call-update
  7.3 1.1 copy.20
  8.4 1.1 copy.21
  9.5 47.8 %all-gather.2.cloned.1.call-done = bf16[1,512,16,128]{3,2,0,1:T(8,128)(2,1)} async-done(((bf16[1,128,16,128]{3,2,0,1:T(8,128)(2,1)}), bf16[1,512,16,128]{3,2,0,1:T(8,128)(2,1)}) %all-gather.2.cloned.1.call-update) | async-done | bytes 2097168 | tf_op jit(solution)/shard_map/all_gather | solution.py:17
  57.3 57.1 %while.13 = (s32[]{:T(128)}, bf16[8,1,64,16,128]{4,3,2,1,0:T(8,128)(2,1)S(1)}, f32[8,1,64,16]{2,0,3,1:T(8,128)S(1)}, s32[8]{0:T(128)S(1)}, s32[1]{0:T(128)}, /*i...) while((s32[]{:T(128)}, ...), condition=%wide.region_3.4_spmd.clone, body=%wide.region_0.3_spmd.clone.sunk | while | flops 550831168 | bytes 15004841 | solution.py:55
  57.3 0.6 dynamic_slice.16
  59.2 0.1 broadcast_compare_fusion.2
  59.3 2.1 %fusion.34 = (f32[2,64,8]{2,1,0:T(8,128)S(1)}, f32[2,64,8,1024]{3,2,1,0:T(8,128)S(1)}) fusion(pred[64,1024]{1,0:T(8,128)(4,1)S(1)} %broadcast_compare_fusion.2, bf16[1,1024,2,128]{3,1,2,0:T(8,128)(2,1)S(1)} %get-tuple-element.220, bf16[8,1,64,16,128]{4,3,2,1,0:T(8,128)(2,1)} %get-tuple-element.219, s32[]{:T(128)} %get-tuple-element.202), kind=kOutput, calls=%fused_computation.3.clone.1 | convolution fusion | flops 271580160 | bytes 5050880 | tf_op jit(solution)/shard_map/while/body/eval_jaxpr/cbkgd,cskd->ckbgs/dot_general | solution.py:29
  61.4 1.5 fusion.35
  62.9 1.3 fusion.36
  64.3 0.1 bitcast_dynamic-update-slice_fusion.2
  64.3 0.1 copy.44
  64.5 0.6 dynamic_slice.16
  66.4 0.1 broadcast_compare_fusion.2
  66.5 2.1 %fusion.34 = (f32[2,64,8]{2,1,0:T(8,128)S(1)}, f32[2,64,8,1024]{3,2,1,0:T(8,128)S(1)}) fusion(pred[64,1024]{1,0:T(8,128)(4,1)S(1)} %broadcast_compare_fusion.2, bf16[1,1024,2,128]{3,1,2,0:T(8,128)(2,1)S(1)} %get-tuple-element.220, bf16[8,1,64,16,128]{4,3,2,1,0:T(8,128)(2,1)} %get-tuple-element.219, s32[]{:T(128)} %get-tuple-element.202), kind=kOutput, calls=%fused_computation.3.clone.1 | convolution fusion | flops 271580160 | bytes 5050880 | tf_op jit(solution)/shard_map/while/body/eval_jaxpr/cbkgd,cskd->ckbgs/dot_general | solution.py:29
  68.6 1.5 fusion.35
  70.1 1.3 fusion.36
  71.4 0.1 bitcast_dynamic-update-slice_fusion.2
  71.5 0.1 copy.44
  71.6 0.6 dynamic_slice.16
  73.5 0.1 broadcast_compare_fusion.2
  73.6 2.1 %fusion.34 = (f32[2,64,8]{2,1,0:T(8,128)S(1)}, f32[2,64,8,1024]{3,2,1,0:T(8,128)S(1)}) fusion(pred[64,1024]{1,0:T(8,128)(4,1)S(1)} %broadcast_compare_fusion.2, bf16[1,1024,2,128]{3,1,2,0:T(8,128)(2,1)S(1)} %get-tuple-element.220, bf16[8,1,64,16,128]{4,3,2,1,0:T(8,128)(2,1)} %get-tuple-element.219, s32[]{:T(128)} %get-tuple-element.202), kind=kOutput, calls=%fused_computation.3.clone.1 | convolution fusion | flops 271580160 | bytes 5050880 | tf_op jit(solution)/shard_map/while/body/eval_jaxpr/cbkgd,cskd->ckbgs/dot_general | solution.py:29
  75.7 1.5 fusion.35
  77.2 1.3 fusion.36
  78.5 0.1 bitcast_dynamic-update-slice_fusion.2
  78.7 0.6 dynamic_slice.16
  80.6 0.1 broadcast_compare_fusion.2
  80.8 2.1 %fusion.34 = (f32[2,64,8]{2,1,0:T(8,128)S(1)}, f32[2,64,8,1024]{3,2,1,0:T(8,128)S(1)}) fusion(pred[64,1024]{1,0:T(8,128)(4,1)S(1)} %broadcast_compare_fusion.2, bf16[1,1024,2,128]{3,1,2,0:T(8,128)(2,1)S(1)} %get-tuple-element.220, bf16[8,1,64,16,128]{4,3,2,1,0:T(8,128)(2,1)} %get-tuple-element.219, s32[]{:T(128)} %get-tuple-element.202), kind=kOutput, calls=%fused_computation.3.clone.1 | convolution fusion | flops 271580160 | bytes 5050880 | tf_op jit(solution)/shard_map/while/body/eval_jaxpr/cbkgd,cskd->ckbgs/dot_general | solution.py:29
  82.9 1.5 fusion.35
  84.4 1.3 fusion.36
  85.7 0.1 bitcast_dynamic-update-slice_fusion.2
  85.8 0.1 copy.44
  85.9 0.6 dynamic_slice.16
  87.8 0.1 broadcast_compare_fusion.2
  87.9 2.1 %fusion.34 = (f32[2,64,8]{2,1,0:T(8,128)S(1)}, f32[2,64,8,1024]{3,2,1,0:T(8,128)S(1)}) fusion(pred[64,1024]{1,0:T(8,128)(4,1)S(1)} %broadcast_compare_fusion.2, bf16[1,1024,2,128]{3,1,2,0:T(8,128)(2,1)S(1)} %get-tuple-element.220, bf16[8,1,64,16,128]{4,3,2,1,0:T(8,128)(2,1)} %get-tuple-element.219, s32[]{:T(128)} %get-tuple-element.202), kind=kOutput, calls=%fused_computation.3.clone.1 | convolution fusion | flops 271580160 | bytes 5050880 | tf_op jit(solution)/shard_map/while/body/eval_jaxpr/cbkgd,cskd->ckbgs/dot_general | solution.py:29
  90.0 1.5 fusion.35
  91.5 1.3 fusion.36
  92.8 0.1 bitcast_dynamic-update-slice_fusion.2
  93.0 0.6 dynamic_slice.16
  94.9 0.1 broadcast_compare_fusion.2
  95.0 2.1 %fusion.34 = (f32[2,64,8]{2,1,0:T(8,128)S(1)}, f32[2,64,8,1024]{3,2,1,0:T(8,128)S(1)}) fusion(pred[64,1024]{1,0:T(8,128)(4,1)S(1)} %broadcast_compare_fusion.2, bf16[1,1024,2,128]{3,1,2,0:T(8,128)(2,1)S(1)} %get-tuple-element.220, bf16[8,1,64,16,128]{4,3,2,1,0:T(8,128)(2,1)} %get-tuple-element.219, s32[]{:T(128)} %get-tuple-element.202), kind=kOutput, calls=%fused_computation.3.clone.1 | convolution fusion | flops 271580160 | bytes 5050880 | tf_op jit(solution)/shard_map/while/body/eval_jaxpr/cbkgd,cskd->ckbgs/dot_general | solution.py:29
  97.1 1.5 fusion.35
  98.6 1.3 fusion.36
  100.0 0.1 bitcast_dynamic-update-slice_fusion.2
  100.2 0.6 dynamic_slice.16
  102.1 0.1 broadcast_compare_fusion.2
  102.2 2.1 %fusion.34 = (f32[2,64,8]{2,1,0:T(8,128)S(1)}, f32[2,64,8,1024]{3,2,1,0:T(8,128)S(1)}) fusion(pred[64,1024]{1,0:T(8,128)(4,1)S(1)} %broadcast_compare_fusion.2, bf16[1,1024,2,128]{3,1,2,0:T(8,128)(2,1)S(1)} %get-tuple-element.220, bf16[8,1,64,16,128]{4,3,2,1,0:T(8,128)(2,1)} %get-tuple-element.219, s32[]{:T(128)} %get-tuple-element.202), kind=kOutput, calls=%fused_computation.3.clone.1 | convolution fusion | flops 271580160 | bytes 5050880 | tf_op jit(solution)/shard_map/while/body/eval_jaxpr/cbkgd,cskd->ckbgs/dot_general | solution.py:29
  104.3 1.5 fusion.35
  105.8 1.3 fusion.36
  107.1 0.1 bitcast_dynamic-update-slice_fusion.2
  107.3 0.6 dynamic_slice.16
  109.2 0.1 broadcast_compare_fusion.2
  109.3 2.1 %fusion.34 = (f32[2,64,8]{2,1,0:T(8,128)S(1)}, f32[2,64,8,1024]{3,2,1,0:T(8,128)S(1)}) fusion(pred[64,1024]{1,0:T(8,128)(4,1)S(1)} %broadcast_compare_fusion.2, bf16[1,1024,2,128]{3,1,2,0:T(8,128)(2,1)S(1)} %get-tuple-element.220, bf16[8,1,64,16,128]{4,3,2,1,0:T(8,128)(2,1)} %get-tuple-element.219, s32[]{:T(128)} %get-tuple-element.202), kind=kOutput, calls=%fused_computation.3.clone.1 | convolution fusion | flops 271580160 | bytes 5050880 | tf_op jit(solution)/shard_map/while/body/eval_jaxpr/cbkgd,cskd->ckbgs/dot_general | solution.py:29
  111.4 1.5 fusion.35
  112.9 1.3 fusion.36
  114.3 0.1 bitcast_dynamic-update-slice_fusion.2
  114.5 0.1 reshape_reshape_transpose.6
  114.6 8.1 %all_to_all.10 = f32[1,4,128,16]{2,3,0,1:T(8,128)S(1)} all-to-all(f32[1,4,128,16]{2,3,0,1:T(8,128)S(1)} %copy.23), channel_id=1, replica_groups=mesh['ctx'=4,'kvh'=4,'conv'=2] {'ctx'}, dimensions={1} | all-to-all | bytes 65536 | tf_op jit(solution)/shard_map/all_to_all | solution.py:70
  122.7 3.6 %all-to-all-start.1 = ((bf16[1,4,128,16,128]{4,3,2,0,1:T(8,128)(2,1)}), bf16[1,4,128,16,128]{4,3,2,0,1:T(8,128)(2,1)S(1)}, u32[]{:S(2)}, u32[]{:S(2)}) async-start(bf16[1,4,128,16,128]{4,3,2,0,1:T(8,128)(2,1)} %bitcast.63), calls=%async_computation.1 | async-start | bytes 4194304 | tf_op jit(solution)/shard_map/all_to_all | solution.py:63
  126.3 0.1 copy.24
  126.5 0.1 copy.26
  126.6 46.9 %all-to-all-done.1 = bf16[1,4,128,16,128]{4,3,2,0,1:T(8,128)(2,1)S(1)} async-done(((bf16[1,4,128,16,128]{4,3,2,0,1:T(8,128)(2,1)}), bf16[1,4,128,16,128]{4,3,2,0,1:T(8,128)(2,1)S(1)}, u32[]{:S(2)}, u32[]{:S(2)}) %all-to-all-start.1) | async-done | bytes 2097184 | tf_op jit(solution)/shard_map/all_to_all | solution.py:63
  173.5 1.5 multiply_reduce_fusion
  175.0 1.1 fusion.24
  (46 shorter events, 0.9 us)
Async XLA Ops:
  6.5 50.8 %all-gather.2.cloned.1.call-start = ((), (), s32[]{:S(2)}) async-start(), calls=%async_computation.2 | async-start | bytes 2621440 | tf_op jit(solution)/shard_map/all_gather | solution.py:17
  114.5 8.2 %copy-start = (bf16[8,1,64,16,128]{4,3,2,1,0:T(8,128)(2,1)}, bf16[8,1,64,16,128]{4,3,2,1,0:T(8,128)(2,1)S(1)}, u32[]{:S(2)}) copy-start(bf16[8,1,64,16,128]{4,3,2,1,0:T(8,128)(2,1)S(1)} %get-tuple-element.54) | copy-start | bytes 6291460
  122.7 50.8 %all-to-all-start.1 = ((bf16[1,4,128,16,128]{4,3,2,0,1:T(8,128)(2,1)}), bf16[1,4,128,16,128]{4,3,2,0,1:T(8,128)(2,1)S(1)}, u32[]{:S(2)}, u32[]{:S(2)}) async-start(bf16[1,4,128,16,128]{4,3,2,0,1:T(8,128)(2,1)} %bitcast.63), calls=%async_computation.1 | async-start | bytes 4194304 | tf_op jit(solution)/shard_map/all_to_all | solution.py:63
Sparse Core Ops, SparseCore 0:
  8.9 48.3 all-gather.1
where the time goes:
time: 184 us; the launch traced here: 183 us
  waiting for transfers between devices  95.4 us (52%)
  matrix products  27.3 us (15%)
  other arithmetic  15.6 us (8%)
  between operations  13.5 us (7%)
  loops' own time  10.6 us (6%)
  local copies, waits for them, and re-layouts  8.89 us (5%)
  blocking collectives  8.11 us (4%)
  starting transfers between devices  3.61 us (2%)
    all_gather x1, waiting for transfers between devices, shards(): piece_rows = lax.all_gather(queries, 'ctx', axis=1, tiled=True)  47.8 us
    all_to_all x1, waiting for transfers between devices, shards(): lax.all_to_all(partial_value.reshape(conv_dev, cycle_size, tok_dev, head_...  46.9 us
    dot_general x8, matrix products, one_block(): jnp.einsum('cbkgd,cskd->ckbgs', query_block, keys, preferred_element_type...  16.8 us
    reduce_sum x8, other arithmetic, one_block(): exp_total = jnp.sum(weights, axis=-1)  11.8 us
    another operation x1, loops' own time, shards(): lax.map(one_block, (blocks, jnp.arange(block_total, dtype=jnp.int32)))  10.6 us
    dot_general x8, matrix products, one_block(): jnp.einsum('ckbgs,cskd->ckbgd', rounded, values, preferred_element_type=j...  10.5 us
    all_to_all x1, blocking collectives, shards(): lax.all_to_all(log_total.reshape(conv_dev, cycle_size, tok_dev, head_dev)...  8.11 us
    dynamic_slice x8, local copies, waits for them, and re-layouts, shards(): lax.map(one_block, (blocks, jnp.arange(block_total, dtype=jnp.int32)))  4.94 us
  transfers between devices with their start and end apart: 2, of which 2 were waited for; matrix products, arithmetic and copies ran while one was open for 1% of the time, Pallas kernels for 0%

commit v1 on v0

--- a/solution.py
+++ b/solution.py
@@ -1,12 +1,205 @@
+import functools
+
 import jax
 import jax.numpy as jnp
 from jax import lax
+from jax.experimental import pallas as pl
+from jax.experimental.pallas import tpu as pltpu
 from jax.sharding import PartitionSpec as P
 
 mask_fill = -1e30
-
-
-def shards(queries, keys, values, lengths):
+empty_max = -1e29
+block_rows = 256
+tail_rows = 32
+
+
+def attend_body(where_ref, q_ref, kv_own_ref, kv_next_ref, out_ref, m_ref, l_ref, acc_ref, lse_ref, *, group, exponent_scale, score_scale):
+    step = pl.program_id(0)
+    rows = m_ref.shape[0]
+    lanes = out_ref.shape[1]
+    keys = kv_own_ref.shape[1]
+    row_tokens = rows // group
+    total_rows = rows * pl.num_programs(0)
+    first = where_ref[0] + step * row_tokens
+    q = q_ref[...].reshape(rows, lanes)
+    m_ref[...] = jnp.full(m_ref.shape, empty_max, jnp.float32)
+    l_ref[...] = jnp.zeros(l_ref.shape, jnp.float32)
+    acc_ref[...] = jnp.zeros(acc_ref.shape, jnp.float32)
+
+    def one_shard(kv_ref, base, masked):
+        scores = lax.dot_general(q, kv_ref[0], (((1,), (1,)), ((), ())), preferred_element_type=jnp.float32)
+        if masked:
+            ahead = lax.broadcasted_iota(jnp.int32, scores.shape, 1) - lax.broadcasted_iota(jnp.int32, scores.shape, 0) // group
+            scores = jnp.where(ahead <= first - base, scores, mask_fill)
+        old = m_ref[...]
+        new = jnp.maximum(old, jnp.max(scores, axis=-1, keepdims=True))
+        alpha = jnp.exp2((old - new) * exponent_scale)
+        weights = jnp.exp2((scores - new[:, :1]) * exponent_scale).astype(jnp.bfloat16)
+        value = kv_ref[1]
+        widened = jnp.concatenate([value, jnp.ones_like(value)], axis=1)
+        mixed = jnp.dot(weights, widened, preferred_element_type=jnp.float32)
+        acc_ref[...] = acc_ref[...] * alpha + mixed[:, :lanes]
+        l_ref[...] = l_ref[...] * alpha + mixed[:, lanes:]
+        m_ref[...] = new
+
+    for slot, kv_ref in ((1, kv_own_ref), (2, kv_next_ref)):
+        base = where_ref[slot]
+        full = first >= base + keys - 1
+        some = first + row_tokens - 1 >= base
+
+        @pl.when(full)
+        def _():
+            one_shard(kv_ref, base, False)
+
+        @pl.when(jnp.logical_and(some, jnp.logical_not(full)))
+        def _():
+            one_shard(kv_ref, base, True)
+
+    total = jnp.maximum(l_ref[...], 1.0)
+    out_ref[pl.ds(pl.multiple_of(step * rows, rows), rows), :] = (acc_ref[...] / total).astype(jnp.bfloat16)
+    lse = m_ref[...] * score_scale + jnp.log(total)
+    diagonal = lax.broadcasted_iota(jnp.int32, (lanes, lanes), 0) == lax.broadcasted_iota(jnp.int32, (lanes, lanes), 1)
+    for part in range(rows // lanes):
+        piece = jnp.where(diagonal, lse[part * lanes : (part + 1) * lanes], 0.0)
+        lse_ref[pl.ds(step * (rows // lanes) + part, 1), :] = jnp.sum(piece, axis=0, keepdims=True)
+
+    @pl.when(step == pl.num_programs(0) - 1)
+    def _():
+        whole = lse_ref[...]
+        high = whole.astype(jnp.bfloat16).astype(jnp.float32)
+        middle = (whole - high).astype(jnp.bfloat16).astype(jnp.float32)
+        low = whole - high - middle
+        tail = jnp.concatenate([high, middle, low, jnp.zeros_like(low)], axis=0)
+        out_ref[out_ref.shape[0] - tail.shape[0] :, :] = tail.astype(jnp.bfloat16)
+
+
+def attend(where, queries, kv_own, kv_next, head, group, name):
+    tok_dev, _, head_dim = queries.shape
+    keys = kv_own.shape[1]
+    total_rows = tok_dev * group
+    rows = min(block_rows, total_rows)
+    lse_rows = total_rows // head_dim
+    body = functools.partial(attend_body, group=group, exponent_scale=1.4426950408889634 / head_dim**0.5, score_scale=1.0 / head_dim**0.5)
+    return pl.pallas_call(
+        body,
+        name=name,
+        out_shape=jax.ShapeDtypeStruct((total_rows + 4 * lse_rows, head_dim), jnp.bfloat16),
+        grid=(total_rows // rows,),
+        in_specs=[
+            pl.BlockSpec(memory_space=pltpu.SMEM),
+            pl.BlockSpec((rows // group, group, head_dim), lambda i: (i, head, 0)),
+            pl.BlockSpec((2, keys, head_dim), lambda i: (0, 0, 0)),
+            pl.BlockSpec((2, keys, head_dim), lambda i: (0, 0, 0)),
+        ],
+        out_specs=pl.BlockSpec((total_rows + 4 * lse_rows, head_dim), lambda i: (0, 0)),
+        scratch_shapes=[
+            pltpu.VMEM((rows, head_dim), jnp.float32),
+            pltpu.VMEM((rows, head_dim), jnp.float32),
+            pltpu.VMEM((rows, head_dim), jnp.float32),
+            pltpu.VMEM((lse_rows, head_dim), jnp.float32),
+        ],
+        cost_estimate=pl.CostEstimate(flops=8 * total_rows * keys * head_dim, transcendentals=2 * total_rows * keys, bytes_accessed=3 * total_rows * head_dim * 2),
+    )(where, queries, kv_own, kv_next)
+
+
+def merge_body(inner_ref, own_refs, near_refs, far_refs, out_ref, w_ref, *, group):
+    step = pl.program_id(0)
+    lanes = out_ref.shape[2]
+    rows = own_refs[0][0].shape[0]
+    row_tokens = rows // group
+    inner = inner_ref[0] > 0
+    diagonal = lax.broadcasted_iota(jnp.int32, (lanes, lanes), 0) == lax.broadcasted_iota(jnp.int32, (lanes, lanes), 1)
+
+    def totals(ref):
+        parts = ref[...].astype(jnp.float32)
+        count = parts.shape[0] // 4
+        return parts[:count] + parts[count : 2 * count] + parts[2 * count : 3 * count]
+
+    for head in range(len(own_refs)):
+        own, own_tail = own_refs[head]
+        near, near_tail = near_refs[head]
+        far, far_tail = far_refs[head]
+        own_total = totals(own_tail)
+        other_total = jnp.where(inner, totals(near_tail), totals(far_tail))
+        top = jnp.maximum(own_total, other_total)
+        own_share = jnp.exp(own_total - top)
+        other_share = jnp.exp(other_total - top)
+        w_ref[...] = other_share / (own_share + other_share)
+        for part in range(rows // lanes):
+            row = w_ref[pl.ds(step * (rows // lanes) + part, 1), :]
+            column = jnp.sum(jnp.where(diagonal, row, 0.0), axis=1, keepdims=True)
+            span = slice(part * lanes, (part + 1) * lanes)
+            mine = own[span, :].astype(jnp.float32)
+            other = jnp.where(inner, near[span, :].astype(jnp.float32), far[span, :].astype(jnp.float32))
+            mixed = (mine + column * (other - mine)).astype(jnp.bfloat16)
+            tokens = lanes // group
+            out_ref[part * tokens : (part + 1) * tokens, head * group : (head + 1) * group, :] = mixed.reshape(tokens, group, lanes)
+
+
+def merge(inner, own, near, far, tok_dev, group):
+    heads = len(own)
+    head_dim = own[0].shape[1]
+    total_rows = tok_dev * group
+    rows = min(block_rows, total_rows)
+    lse_rows = total_rows // head_dim
+    tail = 4 * lse_rows
+
+    def body(inner_ref, *refs):
+        pairs = [(refs[2 * i], refs[2 * i + 1]) for i in range(3 * heads)]
+        merge_body(inner_ref, pairs[:heads], pairs[heads : 2 * heads], pairs[2 * heads :], refs[-2], refs[-1], group=group)
+
+    specs = [pl.BlockSpec((rows, head_dim), lambda i: (i, 0)), pl.BlockSpec((tail, head_dim), lambda i: (total_rows // tail, 0))]
+    operands = [array for array in (*own, *near, *far) for _ in range(2)]
+    return pl.pallas_call(
+        body,
+        name="merge",
+        out_shape=jax.ShapeDtypeStruct((tok_dev, heads * group, head_dim), jnp.bfloat16),
+        grid=(total_rows // rows,),
+        in_specs=[pl.BlockSpec(memory_space=pltpu.SMEM)] + specs * (3 * heads),
+        out_specs=pl.BlockSpec((rows // group, heads * group, head_dim), lambda i: (i, 0, 0)),
+        scratch_shapes=[pltpu.VMEM((lse_rows, head_dim), jnp.float32)],
+    )(inner, *operands)
+
+
+def line_of_pairs(queries, keys, values, lengths):
+    count = lax.axis_size("ctx")
+    half = count // 2
+    index = lax.axis_index("ctx")
+    tok_dev, head_dev, head_dim = queries.shape[1:]
+    ctx_dev, kv_dev = keys.shape[1:3]
+    group = head_dev // kv_dev
+    near_pairs = [(half - 1, half), (half, half - 1)]
+    far_pairs = [(0, half), (count - 1, half - 1)]
+    far_back = [(half, 0), (half - 1, count - 1)]
+    kv_pairs = [(i, i ^ 1) for i in range(count)]
+    mine = queries[0]
+    near = lax.ppermute(mine, "ctx", near_pairs)
+    kv = jnp.stack([jnp.transpose(keys[0], (1, 0, 2)), jnp.transpose(values[0], (1, 0, 2))], axis=1)
+    kv_own = [kv[h] for h in range(kv_dev)]
+    kv_next = [lax.ppermute(kv_own[0], "ctx", kv_pairs)]
+    far = lax.ppermute(mine, "ctx", far_pairs)
+    kv_next += [lax.ppermute(kv_own[h], "ctx", kv_pairs) for h in range(1, kv_dev)]
+
+    length = lengths[0]
+    bases = [index * ctx_dev, (index ^ 1) * ctx_dev]
+
+    def where(owner):
+        return jnp.stack([length + owner * tok_dev, *bases]).astype(jnp.int32)
+
+    near_owner = count - 1 - index
+    far_owner = jnp.where(index >= half, 0, count - 1)
+    own, near_parts, far_parts = [], [], []
+    for h in range(kv_dev):
+        near_part = attend(where(near_owner), near, kv_own[h], kv_next[h], h, group, f"near{h}")
+        near_parts.append(lax.ppermute(near_part, "ctx", near_pairs))
+        far_part = attend(where(far_owner), far, kv_own[h], kv_next[h], h, group, f"far{h}")
+        far_parts.append(lax.ppermute(far_part, "ctx", far_back))
+        own.append(attend(where(index), mine, kv_own[h], kv_next[h], h, group, f"own{h}"))
+    inner = jnp.logical_or(index == half - 1, index == half).astype(jnp.int32).reshape(1)
+    return merge(inner, own, near_parts, far_parts, tok_dev, group)[None]
+
+
+def gathered(queries, keys, values, lengths):
     conv_dev, tok_dev, head_dev, head_dim = queries.shape
     ctx_dev = keys.shape[1]
     kv_dev = keys.shape[2]
@@ -59,7 +252,6 @@
         conv_dev, row_count, head_dev, head_dim
     )
     log_total = jnp.moveaxis(log_total, 0, 1).reshape(conv_dev, row_count, head_dev)
-    partial_value, log_total = (partial_value, log_total)
     arrived = lax.all_to_all(
         partial_value.reshape(conv_dev, cycle_size, tok_dev, head_dev, head_dim),
         "ctx",
@@ -81,6 +273,12 @@
     return (numerator / denominator[..., None]).astype(jnp.bfloat16)
 
 
+def shards(queries, keys, values, lengths):
+    if queries.shape[0] == 1 and lax.axis_size("ctx") == 2 * len(("inner", "outer")):
+        return line_of_pairs(queries, keys, values, lengths)
+    return gathered(queries, keys, values, lengths)
+
+
 def solution(mesh):
     in_specs = (
         P("conv", "ctx", "kvh", None),

time: 184 us -> 94.2 us (0.51)
  the two profiles are of different devices: /device:TPU:0 before, /device:TPU:13 now
where the time goes in v1:
time: 94.2 us; the launch traced here: 92.8 us
  Pallas kernels  66.5 us (71%)
  starting transfers between devices  13.9 us (15%)
  waiting for transfers between devices  5.63 us (6%)
  local copies, waits for them, and re-layouts  4.02 us (4%)
  other arithmetic  1.91 us (2%)
    pallas_call x6, Pallas kernels, attend(): pl.pallas_call(body, name=name, out_shape=jax.ShapeDtypeStruct((total_row...  62.8 us
    ppermute x2, starting transfers between devices, line_of_pairs(): near_parts.append(lax.ppermute(near_part, 'ctx', near_pairs))  4 us
    pallas_call x1, Pallas kernels, merge(): pl.pallas_call(body, name='merge', out_shape=jax.ShapeDtypeStruct((tok_de...  3.68 us
    ppermute x1, waiting for transfers between devices, line_of_pairs(): near = lax.ppermute(mine, 'ctx', near_pairs)  3.25 us
    ppermute x1, starting transfers between devices, line_of_pairs(): near = lax.ppermute(mine, 'ctx', near_pairs)  3.19 us
    ppermute x1, starting transfers between devices, line_of_pairs(): kv_next = [lax.ppermute(kv_own[0], 'ctx', kv_pairs)]  2.79 us
    unnamed x18, local copies, waits for them, and re-layouts  2.68 us
    ppermute x2, starting transfers between devices, line_of_pairs(): far_parts.append(lax.ppermute(far_part, 'ctx', far_back))  2.59 us
  transfers between devices with their start and end apart: 8, of which 2 were waited for; matrix products, arithmetic and copies ran while one was open for 4% of the time, Pallas kernels for 68%

profile of v1, /device:TPU:13, one launch (start us, length us, event | category | flops | bytes accessed | tf_op | source)
XLA Modules:
  0.0 92.8 jit_solution(13070993445951598082)
XLA Ops:
  0.0 3.2 %collective-permute-start.2 = (bf16[128,16,128]{2,1,0:T(8,128)(2,1)}, bf16[128,16,128]{2,1,0:T(8,128)(2,1)S(1)}, u32[]{:S(2)}, u32[]{:S(2)}) collective-permute-start(bf16[128,16,128]{2,1,0:T(8,128)(2,1)} %bitcast.28), channel_id=1, source_target_pairs={{8,16},{16,8},{9,17},{17,9},{10,18},{18,10},{11,19},{19,11},{12,20... | collective-permute-start | bytes 1572872 | tf_op jit(solution)/shard_map/ppermute | solution.py:176
  3.2 1.3 %copy_bitcast_fusion = (bf16[2,1,1024,128]{3,2,1,0:T(8,128)(2,1)S(1)}, bf16[2,1,1024,128]{3,2,1,0:T(8,128)(2,1)S(1)}) fusion(bf16[1,1024,2,128]{3,2,1,0:T(2,128)(2,1)} %param.6, bf16[1,1024,2,128]{3,2,1,0:T(2,128)(2,1)} %param.5), kind=kLoop, calls=%fused_computation.6 | loop fusion | bytes 2097152 | tf_op jit(solution)/shard_map/stack | solution.py:177
  4.5 0.0 copy-start.6
  4.6 0.1 fusion.2
  4.7 0.0 copy-start.5
  4.7 0.0 copy-start.4
  4.7 0.1 collective-permute-start.1
  4.8 0.9 copy-done.6
  5.7 1.3 %collective-permute-start.5 = (bf16[128,16,128]{2,1,0:T(8,128)(2,1)S(1)}, bf16[128,16,128]{2,1,0:T(8,128)(2,1)}, u32[]{:S(2)}, u32[]{:S(2)}) collective-permute-start(bf16[128,16,128]{2,1,0:T(8,128)(2,1)S(1)} %bitcast.31), channel_id=1, source_target_pairs={{0,16},{24,8},{1,17},{25,9},{2,18},{26,10},{3,19},{27,11},{4,20},{... | collective-permute-start | bytes 1572872 | tf_op jit(solution)/shard_map/ppermute | solution.py:180
  6.9 2.8 %collective-permute-start = (bf16[2,1024,128]{2,1,0:T(8,128)(2,1)S(1)}, bf16[2,1024,128]{2,1,0:T(8,128)(2,1)}, u32[]{:S(2)}, u32[]{:S(2)}) collective-permute-start(bf16[2,1024,128]{2,1,0:T(8,128)(2,1)S(1)} %get-tuple-element.6.kv_own_ref), channel_id=1, source_target_pairs={{0,8},{8,0},{16,24},{24,16},{1,9},{9,1},{17,25},{25,17},{2,10},{10... | collective-permute-start | bytes 1572872 | tf_op jit(solution)/shard_map/ppermute | solution.py:179
  10.4 0.6 add_add_fusion.1.where_ref
  11.0 0.7 add_add_fusion.2.where_ref
  11.7 3.3 %collective-permute-done.2.q_ref = bf16[128,16,128]{2,1,0:T(8,128)(2,1)S(1)} collective-permute-done((bf16[128,16,128]{2,1,0:T(8,128)(2,1)}, bf16[128,16,128]{2,1,0:T(8,128)(2,1)S(1)}, u32[]{:S(2)}, u32[]{:S(2)}) %collective-permute-start.2) | collective-permute-done | bytes 524320 | tf_op jit(solution)/shard_map/ppermute | solution.py:176
  14.9 0.0 copy-start.8
  14.9 2.4 %collective-permute-done.1.kv_next_ref = bf16[2,1024,128]{2,1,0:T(8,128)(2,1)S(1)} collective-permute-done((bf16[2,1024,128]{2,1,0:T(8,128)(2,1)S(1)}, bf16[2,1024,128]{2,1,0:T(8,128)(2,1)S(1)}, u32[]{:S(2)}, u32[]{:S(2)}) %collective-permute-start.1) | collective-permute-done | bytes 524320 | tf_op jit(solution)/shard_map/ppermute | solution.py:181
  17.3 0.0 copy-done.5
  17.3 0.0 copy-done.8
  17.3 0.0 copy-start.7
  17.3 0.8 copy-done.7
  18.1 10.5 %near1.1 = bf16[1056,128]{1,0:T(8,128)(2,1)} custom-call(s32[3]{0:T(128)} %add_add_fusion.1.where_ref, bf16[128,16,128]{2,1,0:T(8,128)(2,1)} %copy-done.8, bf16[2,1024,128]{2,1,0:T(8,128)(2,1)} %copy-done.5, bf16[2,1024,128]{2,1,0:T(8,128)(2,1)} %copy-done.7), custom_call_target="tpu_custom_call" | custom-call | flops 1073741824 | bytes 786432 | tf_op jit(solution)/shard_map/near1/pallas_call | solution.py:83
  28.6 0.0 copy-done.4
  28.6 1.9 %collective-permute-start.4 = (bf16[1056,128]{1,0:T(8,128)(2,1)}, bf16[1056,128]{1,0:T(8,128)(2,1)S(1)}, u32[]{:S(2)}, u32[]{:S(2)}) collective-permute-start(bf16[1056,128]{1,0:T(8,128)(2,1)} %near1.1), channel_id=1, source_target_pairs={{8,16},{16,8},{9,17},{17,9},{10,18},{18,10},{11,19},{19,11},{12,20... | collective-permute-start | bytes 811016 | tf_op jit(solution)/shard_map/ppermute | solution.py:194
  30.5 0.0 collective-permute-done.5.q_ref
  30.5 10.5 %far1.1 = bf16[1056,128]{1,0:T(8,128)(2,1)} custom-call(s32[3]{0:T(128)} %add_add_fusion.2.where_ref, bf16[128,16,128]{2,1,0:T(8,128)(2,1)} %collective-permute-done.5.q_ref, bf16[2,1024,128]{2,1,0:T(8,128)(2,1)} %copy-done.5, bf16[2,1024,128]{2,1,0:T(8,128)(2,1)} %copy-done.7), custom_call_target="tpu_custom_call" | custom-call | flops 1073741824 | bytes 786432 | tf_op jit(solution)/shard_map/far1/pallas_call | solution.py:83
  41.0 1.3 %collective-permute-start.7 = (bf16[1056,128]{1,0:T(8,128)(2,1)}, bf16[1056,128]{1,0:T(8,128)(2,1)S(1)}, u32[]{:S(2)}, u32[]{:S(2)}) collective-permute-start(bf16[1056,128]{1,0:T(8,128)(2,1)} %far1.1), channel_id=1, source_target_pairs={{16,0},{8,24},{17,1},{9,25},{18,2},{10,26},{19,3},{11,27},{20,4},{... | collective-permute-start | bytes 811016 | tf_op jit(solution)/shard_map/ppermute | solution.py:196
  42.3 0.0 collective-permute-done.kv_next_ref
  42.3 10.5 %near0.1 = bf16[1056,128]{1,0:T(8,128)(2,1)} custom-call(s32[3]{0:T(128)} %add_add_fusion.1.where_ref, bf16[128,16,128]{2,1,0:T(8,128)(2,1)} %copy-done.8, bf16[2,1024,128]{2,1,0:T(8,128)(2,1)} %copy-done.4, bf16[2,1024,128]{2,1,0:T(8,128)(2,1)} %collective-permute-done.kv_next_ref), custom_call_target="tpu_custom_call" | custom-call | flops 1073741824 | bytes 786432 | tf_op jit(solution)/shard_map/near0/pallas_call | solution.py:83
  52.8 2.1 %collective-permute-start.3 = (bf16[1056,128]{1,0:T(8,128)(2,1)}, bf16[1056,128]{1,0:T(8,128)(2,1)S(1)}, u32[]{:S(2)}, u32[]{:S(2)}) collective-permute-start(bf16[1056,128]{1,0:T(8,128)(2,1)} %near0.1), channel_id=1, source_target_pairs={{8,16},{16,8},{9,17},{17,9},{10,18},{18,10},{11,19},{19,11},{12,20... | collective-permute-start | bytes 811016 | tf_op jit(solution)/shard_map/ppermute | solution.py:194
  54.8 10.5 %far0.1 = bf16[1056,128]{1,0:T(8,128)(2,1)} custom-call(s32[3]{0:T(128)} %add_add_fusion.2.where_ref, bf16[128,16,128]{2,1,0:T(8,128)(2,1)} %collective-permute-done.5.q_ref, bf16[2,1024,128]{2,1,0:T(8,128)(2,1)} %copy-done.4, bf16[2,1024,128]{2,1,0:T(8,128)(2,1)} %collective-permute-done.kv_next_ref), custom_call_target="tpu_custom_call" | custom-call | flops 1073741824 | bytes 786432 | tf_op jit(solution)/shard_map/far0/pallas_call | solution.py:83
  65.3 1.3 %collective-permute-start.6 = (bf16[1056,128]{1,0:T(8,128)(2,1)}, bf16[1056,128]{1,0:T(8,128)(2,1)S(1)}, u32[]{:S(2)}, u32[]{:S(2)}) collective-permute-start(bf16[1056,128]{1,0:T(8,128)(2,1)} %far0.1), channel_id=1, source_target_pairs={{16,0},{8,24},{17,1},{9,25},{18,2},{10,26},{19,3},{11,27},{20,4},{... | collective-permute-start | bytes 811016 | tf_op jit(solution)/shard_map/ppermute | solution.py:196
  66.6 0.6 add_add_fusion.where_ref
  67.2 10.5 %own1.1.refs_2_.refs_3_ = bf16[1056,128]{1,0:T(8,128)(2,1)} custom-call(s32[3]{0:T(128)} %add_add_fusion.where_ref, bf16[128,16,128]{2,1,0:T(8,128)(2,1)} %bitcast.29, bf16[2,1024,128]{2,1,0:T(8,128)(2,1)} %copy-done.5, bf16[2,1024,128]{2,1,0:T(8,128)(2,1)} %copy-done.7), custom_call_target="tpu_custom_call" | custom-call | flops 1073741824 | bytes 786432 | tf_op jit(solution)/shard_map/own1/pallas_call | solution.py:83
  77.6 10.5 %own0.1.refs_0_.refs_1_ = bf16[1056,128]{1,0:T(8,128)(2,1)} custom-call(s32[3]{0:T(128)} %add_add_fusion.where_ref, bf16[128,16,128]{2,1,0:T(8,128)(2,1)} %bitcast.30, bf16[2,1024,128]{2,1,0:T(8,128)(2,1)} %copy-done.4, bf16[2,1024,128]{2,1,0:T(8,128)(2,1)} %collective-permute-done.kv_next_ref), custom_call_target="tpu_custom_call" | custom-call | flops 1073741824 | bytes 786432 | tf_op jit(solution)/shard_map/own0/pallas_call | solution.py:83
  88.1 0.0 collective-permute-done.4.refs_6_.refs_7_
  88.1 0.0 copy-start
  88.1 0.0 collective-permute-done.7.refs_10_.refs_11_
  88.1 0.0 copy-start.1
  88.1 0.0 collective-permute-done.3.refs_4_.refs_5_
  88.1 0.0 copy-start.2
  88.1 0.0 collective-permute-done.6.refs_8_.refs_9_
  88.1 0.0 copy-start.3
  88.2 0.6 copy-done
  88.8 0.1 copy-done.1
  88.9 0.1 copy-done.2
  89.0 0.1 copy-done.3
  89.1 3.7 %merge.1 = bf16[128,16,128]{2,1,0:T(8,128)(2,1)} custom-call(s32[1]{0:T(128)} %bitcast.inner_ref, bf16[1056,128]{1,0:T(8,128)(2,1)} %own0.1.refs_0_.refs_1_, bf16[1056,128]{1,0:T(8,128)(2,1)} %own0.1.refs_0_.refs_1_, bf16[1056,128]{1,0:T(8,128)(2,1)} %own1.1.refs_2_.refs_3_, bf16[1056,128]{1,0:T(8,128)(2,1)} %own1.1.refs_2_.refs_3_, ...), custom_call_target="tpu_custom_call" | custom-call | tf_op jit(solution)/shard_map/merge/pallas_call | solution.py:153
Async XLA Ops:
  0.0 14.9 %collective-permute-start.2 = (bf16[128,16,128]{2,1,0:T(8,128)(2,1)}, bf16[128,16,128]{2,1,0:T(8,128)(2,1)S(1)}, u32[]{:S(2)}, u32[]{:S(2)}) collective-permute-start(bf16[128,16,128]{2,1,0:T(8,128)(2,1)} %bitcast.28), channel_id=1, source_target_pairs={{8,16},{16,8},{9,17},{17,9},{10,18},{18,10},{11,19},{19,11},{12,20... | collective-permute-start | bytes 1572872 | tf_op jit(solution)/shard_map/ppermute | solution.py:176
  4.5 1.1 %copy-start.6 = (bf16[1,128,16,128]{3,2,1,0:T(8,128)(2,1)S(1)}, bf16[1,128,16,128]{3,2,1,0:T(8,128)(2,1)}, u32[]{:S(2)}) copy-start(bf16[1,128,16,128]{3,2,1,0:T(8,128)(2,1)} %param.4) | copy-start | bytes 1572868
  4.7 12.6 %copy-start.5 = (bf16[2,1024,128]{2,1,0:T(8,128)(2,1)}, bf16[2,1024,128]{2,1,0:T(8,128)(2,1)S(1)}, u32[]{:S(2)}) copy-start(bf16[2,1024,128]{2,1,0:T(8,128)(2,1)S(1)} %get-tuple-element.5.kv_own_ref) | copy-start | bytes 1572868
  4.7 23.9 %copy-start.4 = (bf16[2,1024,128]{2,1,0:T(8,128)(2,1)}, bf16[2,1024,128]{2,1,0:T(8,128)(2,1)S(1)}, u32[]{:S(2)}) copy-start(bf16[2,1024,128]{2,1,0:T(8,128)(2,1)S(1)} %get-tuple-element.6.kv_own_ref) | copy-start | bytes 1572868
  4.7 12.6 %collective-permute-start.1 = (bf16[2,1024,128]{2,1,0:T(8,128)(2,1)S(1)}, bf16[2,1024,128]{2,1,0:T(8,128)(2,1)S(1)}, u32[]{:S(2)}, u32[]{:S(2)}) collective-permute-start(bf16[2,1024,128]{2,1,0:T(8,128)(2,1)S(1)} %get-tuple-element.5.kv_own_ref), channel_id=1, source_target_pairs={{0,8},{8,0},{16,24},{24,16},{1,9},{9,1},{17,25},{25,17},{2,10},{10... | collective-permute-start | bytes 1572872 | tf_op jit(solution)/shard_map/ppermute | solution.py:181
  5.7 24.8 %collective-permute-start.5 = (bf16[128,16,128]{2,1,0:T(8,128)(2,1)S(1)}, bf16[128,16,128]{2,1,0:T(8,128)(2,1)}, u32[]{:S(2)}, u32[]{:S(2)}) collective-permute-start(bf16[128,16,128]{2,1,0:T(8,128)(2,1)S(1)} %bitcast.31), channel_id=1, source_target_pairs={{0,16},{24,8},{1,17},{25,9},{2,18},{26,10},{3,19},{27,11},{4,20},{... | collective-permute-start | bytes 1572872 | tf_op jit(solution)/shard_map/ppermute | solution.py:180
  6.9 35.3 %collective-permute-start = (bf16[2,1024,128]{2,1,0:T(8,128)(2,1)S(1)}, bf16[2,1024,128]{2,1,0:T(8,128)(2,1)}, u32[]{:S(2)}, u32[]{:S(2)}) collective-permute-start(bf16[2,1024,128]{2,1,0:T(8,128)(2,1)S(1)} %get-tuple-element.6.kv_own_ref), channel_id=1, source_target_pairs={{0,8},{8,0},{16,24},{24,16},{1,9},{9,1},{17,25},{25,17},{2,10},{10... | collective-permute-start | bytes 1572872 | tf_op jit(solution)/shard_map/ppermute | solution.py:179
  14.9 2.4 %copy-start.8 = (bf16[128,16,128]{2,1,0:T(8,128)(2,1)}, bf16[128,16,128]{2,1,0:T(8,128)(2,1)S(1)}, u32[]{:S(2)}) copy-start(bf16[128,16,128]{2,1,0:T(8,128)(2,1)S(1)} %collective-permute-done.2.q_ref) | copy-start | bytes 1572868
  17.3 0.8 copy-start.7
  28.6 59.5 %collective-permute-start.4 = (bf16[1056,128]{1,0:T(8,128)(2,1)}, bf16[1056,128]{1,0:T(8,128)(2,1)S(1)}, u32[]{:S(2)}, u32[]{:S(2)}) collective-permute-start(bf16[1056,128]{1,0:T(8,128)(2,1)} %near1.1), channel_id=1, source_target_pairs={{8,16},{16,8},{9,17},{17,9},{10,18},{18,10},{11,19},{19,11},{12,20... | collective-permute-start | bytes 811016 | tf_op jit(solution)/shard_map/ppermute | solution.py:194
  41.0 47.2 %collective-permute-start.7 = (bf16[1056,128]{1,0:T(8,128)(2,1)}, bf16[1056,128]{1,0:T(8,128)(2,1)S(1)}, u32[]{:S(2)}, u32[]{:S(2)}) collective-permute-start(bf16[1056,128]{1,0:T(8,128)(2,1)} %far1.1), channel_id=1, source_target_pairs={{16,0},{8,24},{17,1},{9,25},{18,2},{10,26},{19,3},{11,27},{20,4},{... | collective-permute-start | bytes 811016 | tf_op jit(solution)/shard_map/ppermute | solution.py:196
  52.8 35.4 %collective-permute-start.3 = (bf16[1056,128]{1,0:T(8,128)(2,1)}, bf16[1056,128]{1,0:T(8,128)(2,1)S(1)}, u32[]{:S(2)}, u32[]{:S(2)}) collective-permute-start(bf16[1056,128]{1,0:T(8,128)(2,1)} %near0.1), channel_id=1, source_target_pairs={{8,16},{16,8},{9,17},{17,9},{10,18},{18,10},{11,19},{19,11},{12,20... | collective-permute-start | bytes 811016 | tf_op jit(solution)/shard_map/ppermute | solution.py:194
  65.3 22.8 %collective-permute-start.6 = (bf16[1056,128]{1,0:T(8,128)(2,1)}, bf16[1056,128]{1,0:T(8,128)(2,1)S(1)}, u32[]{:S(2)}, u32[]{:S(2)}) collective-permute-start(bf16[1056,128]{1,0:T(8,128)(2,1)} %far0.1), channel_id=1, source_target_pairs={{16,0},{8,24},{17,1},{9,25},{18,2},{10,26},{19,3},{11,27},{20,4},{... | collective-permute-start | bytes 811016 | tf_op jit(solution)/shard_map/ppermute | solution.py:196
  88.1 0.7 copy-start
  88.1 0.8 copy-start.1
  88.1 0.9 copy-start.2
  88.1 0.9 %copy-start.3 = (bf16[1056,128]{1,0:T(8,128)(2,1)}, bf16[1056,128]{1,0:T(8,128)(2,1)S(1)}, u32[]{:S(2)}) copy-start(bf16[1056,128]{1,0:T(8,128)(2,1)S(1)} %collective-permute-done.6.refs_8_.refs_9_) | copy-start | bytes 811012

commit v2 on v0

--- a/solution.py
+++ b/solution.py
@@ -1,12 +1,215 @@
+import functools
+
 import jax
 import jax.numpy as jnp
 from jax import lax
+from jax.experimental import pallas as pl
+from jax.experimental.pallas import tpu as pltpu
 from jax.sharding import PartitionSpec as P
 
 mask_fill = -1e30
-
-
-def shards(queries, keys, values, lengths):
+empty_max = -1e29
+log2_e = 1.4426950408889634
+kernel_vmem = 20 * 2**20
+
+
+def identity_mask(lanes):
+    return lax.broadcasted_iota(jnp.int32, (lanes, lanes), 0) == lax.broadcasted_iota(jnp.int32, (lanes, lanes), 1)
+
+
+def owner_of(kind, index, count):
+    if kind == "own":
+        return index
+    if kind == "near":
+        return count - 1 - index
+    return jnp.where(index >= count // 2, 0, count - 1)
+
+
+def attend_body(length_ref, q_ref, kv_own_ref, kv_next_ref, out_ref, even_ref, odd_ref, *, kind, head, group, rows, tile, scale, count):
+    lanes = out_ref.shape[1]
+    keys = kv_own_ref.shape[1]
+    tok_dev = q_ref.shape[0]
+    total_rows = tok_dev * group
+    blocks = total_rows // rows
+    row_tokens = rows // group
+    index = lax.axis_index("ctx")
+    first = length_ref[0] + owner_of(kind, index, count) * tok_dev
+    sources = ((kv_own_ref, index * keys), (kv_next_ref, (index ^ 1) * keys))
+    scores_refs = (even_ref, odd_ref)
+    all_keys = len(sources) * keys
+    offset = lax.broadcasted_iota(jnp.int32, (rows, lanes), 0) // group - lax.broadcasted_iota(jnp.int32, (rows, lanes), 1)
+    diagonal = identity_mask(lanes)
+
+    def score(block):
+        q = q_ref[block * row_tokens : (block + 1) * row_tokens, head * group : (head + 1) * group, :].reshape(rows, lanes)
+        top = jnp.full((rows, lanes), empty_max, jnp.float32)
+        for slot, (kv_ref, base) in enumerate(sources):
+            reach = offset + (first + block * row_tokens - base)
+            for start in range(0, keys, tile):
+                raw = lax.dot_general(
+                    q, kv_ref[0, start : start + tile, :], (((1,), (1,)), ((), ())), preferred_element_type=jnp.float32
+                )
+                for lane in range(0, tile, lanes):
+                    masked = jnp.where(reach >= start + lane, raw[:, lane : lane + lanes], mask_fill)
+                    top = jnp.maximum(top, masked)
+                    place = slot * keys + start + lane
+                    scores_refs[block % 2][:, place : place + lanes] = masked
+                yield None
+        yield jnp.broadcast_to(jnp.max(top, axis=-1, keepdims=True), (rows, lanes))
+
+    def mix(block, top):
+        mixed = None
+        for slot, (kv_ref, _) in enumerate(sources):
+            pieces = []
+            for start in range(slot * keys, (slot + 1) * keys, tile):
+                for lane in range(start, start + tile, lanes):
+                    weights = jnp.exp2((scores_refs[block % 2][:, lane : lane + lanes] - top) * (scale * log2_e))
+                    pieces.append(weights.astype(jnp.bfloat16))
+                yield None
+            value = kv_ref[1]
+            widened = jnp.concatenate([value, jnp.ones_like(value)], axis=1)
+            product = jnp.dot(jnp.concatenate(pieces, axis=1), widened, preferred_element_type=jnp.float32)
+            mixed = product if mixed is None else mixed + product
+        total = jnp.maximum(mixed[:, lanes:], 1.0)
+        out_ref[block * rows : (block + 1) * rows, :] = (mixed[:, :lanes] / total).astype(jnp.bfloat16)
+        log_total = top * scale + jnp.log(total)
+        yield [
+            jnp.sum(jnp.where(diagonal, log_total[part : part + lanes], 0.0), axis=0, keepdims=True)
+            for part in range(0, rows, lanes)
+        ]
+
+    top, totals = None, []
+    for block in range(blocks + 1):
+        ahead = score(block) if block < blocks else iter(())
+        behind = mix(block - 1, top) if block > 0 else iter(())
+        running = [ahead, behind]
+        last = {}
+        while running:
+            for stream in list(running):
+                try:
+                    last[id(stream)] = next(stream)
+                except StopIteration:
+                    running.remove(stream)
+        top = last.get(id(ahead))
+        totals += last.get(id(behind), [])
+    whole = jnp.concatenate(totals, axis=0)
+    high = whole.astype(jnp.bfloat16).astype(jnp.float32)
+    middle = (whole - high).astype(jnp.bfloat16).astype(jnp.float32)
+    low = whole - high - middle
+    tail = jnp.concatenate([high, middle, low, jnp.zeros_like(low)], axis=0)
+    out_ref[total_rows:, :] = tail.astype(jnp.bfloat16)
+
+
+def on_chip(array):
+    return pltpu.with_memory_space_constraint(array, pltpu.VMEM)
+
+
+def attend(length, queries, kv_own, kv_next, kind, head, group, count):
+    tok_dev, _, head_dim = queries.shape
+    keys = kv_own.shape[1]
+    total_rows = tok_dev * group
+    rows = min(256, total_rows)
+    body = functools.partial(
+        attend_body, kind=kind, head=head, group=group, rows=rows, tile=min(256, keys), scale=1.0 / head_dim**0.5, count=count
+    )
+    vmem = pl.BlockSpec(memory_space=pltpu.VMEM)
+    return pl.pallas_call(
+        body,
+        name=f"{kind}{head}",
+        out_shape=pltpu.VMEM((total_rows + 4 * total_rows // head_dim, head_dim), jnp.bfloat16),
+        in_specs=[pl.BlockSpec(memory_space=pltpu.SMEM), vmem, vmem, vmem],
+        out_specs=vmem,
+        scratch_shapes=[pltpu.VMEM((rows, 2 * keys), jnp.float32)] * 2,
+        compiler_params=pltpu.CompilerParams(vmem_limit_bytes=kernel_vmem),
+        cost_estimate=pl.CostEstimate(
+            flops=8 * total_rows * keys * head_dim,
+            transcendentals=2 * total_rows * keys,
+            bytes_accessed=2 * head_dim * (2 * total_rows + 4 * keys),
+        ),
+    )(length, on_chip(queries), on_chip(kv_own), on_chip(kv_next))
+
+
+def merge_body(*refs, heads, group, half):
+    own_refs, near_refs, far_refs, out_ref = refs[:heads], refs[heads : 2 * heads], refs[2 * heads : 3 * heads], refs[-1]
+    tok_dev, _, lanes = out_ref.shape
+    total_rows = tok_dev * group
+    count = total_rows // lanes
+    index = lax.axis_index("ctx")
+    inner = jnp.logical_or(index == half - 1, index == half)
+    diagonal = identity_mask(lanes)
+
+    def totals(ref):
+        parts = ref[total_rows:, :].astype(jnp.float32)
+        return parts[:count] + parts[count : 2 * count] + parts[2 * count : 3 * count]
+
+    def combine(other_refs):
+        for head in range(heads):
+            own_total = totals(own_refs[head])
+            other_total = totals(other_refs[head])
+            top = jnp.maximum(own_total, other_total)
+            own_share = jnp.exp(own_total - top)
+            other_share = jnp.exp(other_total - top)
+            portion = other_share / (own_share + other_share)
+            for part in range(count):
+                column = jnp.sum(jnp.where(diagonal, portion[part : part + 1], 0.0), axis=1, keepdims=True)
+                span = slice(part * lanes, (part + 1) * lanes)
+                mine = own_refs[head][span, :].astype(jnp.float32)
+                other = other_refs[head][span, :].astype(jnp.float32)
+                mixed = (mine + column * (other - mine)).astype(jnp.bfloat16)
+                tokens = lanes // group
+                out_ref[part * tokens : (part + 1) * tokens, head * group : (head + 1) * group, :] = mixed.reshape(tokens, group, lanes)
+
+    @pl.when(inner)
+    def _():
+        combine(near_refs)
+
+    @pl.when(jnp.logical_not(inner))
+    def _():
+        combine(far_refs)
+
+
+def merge(own, near, far, tok_dev, group, half):
+    heads = len(own)
+    head_dim = own[0].shape[1]
+    vmem = pl.BlockSpec(memory_space=pltpu.VMEM)
+    return pl.pallas_call(
+        functools.partial(merge_body, heads=heads, group=group, half=half),
+        name="merge",
+        out_shape=jax.ShapeDtypeStruct((tok_dev, heads * group, head_dim), jnp.bfloat16),
+        in_specs=[vmem] * (3 * heads),
+        out_specs=vmem,
+        compiler_params=pltpu.CompilerParams(vmem_limit_bytes=kernel_vmem),
+    )(*map(on_chip, (*own, *near, *far)))
+
+
+def line_of_pairs(queries, keys, values, lengths):
+    count = lax.axis_size("ctx")
+    half = count // 2
+    tok_dev, head_dev, head_dim = queries.shape[1:]
+    kv_dev = keys.shape[2]
+    group = head_dev // kv_dev
+    near_pairs = [(half - 1, half), (half, half - 1)]
+    far_pairs = [(0, half), (count - 1, half - 1)]
+    far_back = [(half, 0), (half - 1, count - 1)]
+    kv_pairs = [(i, i ^ 1) for i in range(count)]
+    mine = queries[0]
+    near = lax.ppermute(mine, "ctx", near_pairs)
+    kv = jnp.stack([jnp.transpose(keys[0], (1, 0, 2)), jnp.transpose(values[0], (1, 0, 2))], axis=1)
+    kv_own = [kv[h] for h in range(kv_dev)]
+    kv_next = [lax.ppermute(kv_own[0], "ctx", kv_pairs)]
+    far = lax.ppermute(mine, "ctx", far_pairs)
+    kv_next += [lax.ppermute(kv_own[h], "ctx", kv_pairs) for h in range(1, kv_dev)]
+    own, near_parts, far_parts = [], [], []
+    for h in range(kv_dev):
+        near_part = attend(lengths, near, kv_own[h], kv_next[h], "near", h, group, count)
+        near_parts.append(lax.ppermute(near_part, "ctx", near_pairs))
+        far_part = attend(lengths, far, kv_own[h], kv_next[h], "far", h, group, count)
+        far_parts.append(lax.ppermute(far_part, "ctx", far_back))
+        own.append(attend(lengths, mine, kv_own[h], kv_next[h], "own", h, group, count))
+    return merge(own, near_parts, far_parts, tok_dev, group, half)[None]
+
+
+def gathered(queries, keys, values, lengths):
     conv_dev, tok_dev, head_dev, head_dim = queries.shape
     ctx_dev = keys.shape[1]
     kv_dev = keys.shape[2]
@@ -59,7 +262,6 @@
         conv_dev, row_count, head_dev, head_dim
     )
     log_total = jnp.moveaxis(log_total, 0, 1).reshape(conv_dev, row_count, head_dev)
-    partial_value, log_total = (partial_value, log_total)
     arrived = lax.all_to_all(
         partial_value.reshape(conv_dev, cycle_size, tok_dev, head_dev, head_dim),
         "ctx",
@@ -81,6 +283,12 @@
     return (numerator / denominator[..., None]).astype(jnp.bfloat16)
 
 
+def shards(queries, keys, values, lengths):
+    if queries.shape[0] == 1 and lax.axis_size("ctx") == 2 * len(("inner", "outer")):
+        return line_of_pairs(queries, keys, values, lengths)
+    return gathered(queries, keys, values, lengths)
+
+
 def solution(mesh):
     in_specs = (
         P("conv", "ctx", "kvh", None),

time: 184 us -> 62.8 us (0.34)
  waiting for transfers between devices: 95.4 us -> 26.4 us
  matrix products: 27.3 us -> 0 us
  Pallas kernels: 0 us -> 20.4 us
  other arithmetic: 15.6 us -> 0.09 us
  between operations: 13.5 us -> 0.76 us
  loops' own time: 10.6 us -> 0 us
  starting transfers between devices: 3.61 us -> 13.5 us
  blocking collectives: 8.11 us -> 0 us
  local copies, waits for them, and re-layouts: 8.89 us -> 1.34 us
    all_gather x1 -> x0, waiting for transfers between devices: 47.8 us -> none  [shards(): piece_rows = lax.all_gather(queries, 'ctx', axis=1, tiled=True)]
    all_to_all x1 -> x0, waiting for transfers between devices: 46.9 us -> none  [shards(): lax.all_to_all(partial_value.reshape(conv_dev, cycle_size, tok_dev, head_...]
    dot_general x16 -> x0, matrix products: 27.3 us -> none  [the longest x8 16.8 us: one_block(): jnp.einsum('cbkgd,cskd->ckbgs', query_block, keys, preferred_element_type...]
    ppermute x0 -> x8, waiting for transfers between devices: none -> 26.4 us  [the longest x1 9.35 us: line_of_pairs(): lax.ppermute(kv_own[h], 'ctx', kv_pairs)]
    pallas_call x0 -> x7, Pallas kernels: none -> 20.4 us  [the longest x6 19.3 us: attend(): pl.pallas_call(body, name=f'{kind}{head}', out_shape=pltpu.VMEM((total_ro...]
    ppermute x0 -> x8, starting transfers between devices: none -> 13.5 us  [the longest x1 5.91 us: line_of_pairs(): lax.ppermute(kv_own[h], 'ctx', kv_pairs)]
    reduce_sum x10 -> x0, other arithmetic: 13.4 us -> none  [the longest x8 11.8 us: one_block(): exp_total = jnp.sum(weights, axis=-1)]
    another operation x1 -> x0, loops' own time: 10.6 us -> none  [shards(): lax.map(one_block, (blocks, jnp.arange(block_total, dtype=jnp.int32)))]
  transfers between devices with their start and end apart: 2 -> 8, of which waited for: 2 -> 4; matrix products, arithmetic and copies ran while one was open for 1% -> 2% of each run, Pallas kernels for 0% -> 31%
where the time goes in v2:
time: 62.8 us; the launch traced here: 62.5 us
  waiting for transfers between devices  26.4 us (42%)
  Pallas kernels  20.4 us (32%)
  starting transfers between devices  13.5 us (21%)
  local copies, waits for them, and re-layouts  1.34 us (2%)
  between operations  0.76 us (1%)
    pallas_call x6, Pallas kernels, attend(): pl.pallas_call(body, name=f'{kind}{head}', out_shape=pltpu.VMEM((total_ro...  19.3 us
    ppermute x1, waiting for transfers between devices, line_of_pairs(): lax.ppermute(kv_own[h], 'ctx', kv_pairs)  9.35 us
    ppermute x1, waiting for transfers between devices, line_of_pairs(): far = lax.ppermute(mine, 'ctx', far_pairs)  6.94 us
    ppermute x1, starting transfers between devices, line_of_pairs(): lax.ppermute(kv_own[h], 'ctx', kv_pairs)  5.91 us
    ppermute x1, waiting for transfers between devices, line_of_pairs(): kv_next = [lax.ppermute(kv_own[0], 'ctx', kv_pairs)]  5.33 us
    ppermute x2, waiting for transfers between devices, line_of_pairs(): far_parts.append(lax.ppermute(far_part, 'ctx', far_back))  4.8 us
    ppermute x1, starting transfers between devices, line_of_pairs(): far = lax.ppermute(mine, 'ctx', far_pairs)  2.67 us
    ppermute x2, starting transfers between devices, line_of_pairs(): far_parts.append(lax.ppermute(far_part, 'ctx', far_back))  2.58 us
  transfers between devices with their start and end apart: 8, of which 4 were waited for; matrix products, arithmetic and copies ran while one was open for 2% of the time, Pallas kernels for 31%

profile of v2, /device:TPU:0, one launch (start us, length us, event | category | flops | bytes accessed | tf_op | source)
XLA Modules:
  0.0 62.5 jit_solution(3440290195310773178)
XLA Ops:
  0.0 0.7 %collective-permute-start.2 = (bf16[128,16,128]{2,1,0:T(8,128)(2,1)}, bf16[128,16,128]{2,1,0:T(8,128)(2,1)S(1)}, u32[]{:S(2)}, u32[]{:S(2)}) collective-permute-start(bf16[128,16,128]{2,1,0:T(8,128)(2,1)} %bitcast.18), channel_id=1, source_target_pairs={{8,16},{16,8},{9,17},{17,9},{10,18},{18,10},{11,19},{19,11},{12,20... | collective-permute-start | bytes 1572872 | tf_op jit(solution)/shard_map/ppermute | solution.py:196
  0.7 1.3 %copy_bitcast_fusion = (bf16[2,1,1024,128]{3,2,1,0:T(8,128)(2,1)S(1)}, bf16[2,1,1024,128]{3,2,1,0:T(8,128)(2,1)S(1)}) fusion(bf16[1,1024,2,128]{3,2,1,0:T(2,128)(2,1)} %param.6, bf16[1,1024,2,128]{3,2,1,0:T(2,128)(2,1)} %param.5), kind=kLoop, calls=%fused_computation.6 | loop fusion | bytes 2097152 | tf_op jit(solution)/shard_map/stack | solution.py:197
  2.0 0.0 copy-start
  2.0 0.1 fusion.2
  2.1 5.9 %collective-permute-start.1 = (bf16[2,1024,128]{2,1,0:T(8,128)(2,1)S(1)}, bf16[2,1024,128]{2,1,0:T(8,128)(2,1)S(1)}, u32[]{:S(2)}, u32[]{:S(2)}) collective-permute-start(bf16[2,1024,128]{2,1,0:T(8,128)(2,1)S(1)} %get-tuple-element.5.kv_own_ref), channel_id=1, source_target_pairs={{0,8},{8,0},{16,24},{24,16},{1,9},{9,1},{17,25},{25,17},{2,10},{10... | collective-permute-start | bytes 1572872 | tf_op jit(solution)/shard_map/ppermute | solution.py:201
  8.1 0.0 copy-done
  8.1 2.7 %collective-permute-start.5 = (bf16[128,16,128]{2,1,0:T(8,128)(2,1)S(1)}, bf16[128,16,128]{2,1,0:T(8,128)(2,1)S(1)}, u32[]{:S(2)}, u32[]{:S(2)}) collective-permute-start(bf16[128,16,128]{2,1,0:T(8,128)(2,1)S(1)} %bitcast.19), channel_id=1, source_target_pairs={{0,16},{24,8},{1,17},{25,9},{2,18},{26,10},{3,19},{27,11},{4,20},{... | collective-permute-start | bytes 1572872 | tf_op jit(solution)/shard_map/ppermute | solution.py:200
  10.7 0.1 collective-permute-start
  11.5 0.0 collective-permute-done.2.q_ref
  11.5 9.4 %collective-permute-done.1.kv_next_ref = bf16[2,1024,128]{2,1,0:T(8,128)(2,1)S(1)} collective-permute-done((bf16[2,1024,128]{2,1,0:T(8,128)(2,1)S(1)}, bf16[2,1024,128]{2,1,0:T(8,128)(2,1)S(1)}, u32[]{:S(2)}, u32[]{:S(2)}) %collective-permute-start.1) | collective-permute-done | bytes 524320 | tf_op jit(solution)/shard_map/ppermute | solution.py:201
  20.8 3.2 %near1.1 = bf16[1056,128]{1,0:T(8,128)(2,1)S(1)} custom-call(s32[1]{0:T(128)S(6)} %copy.9.length_ref, bf16[128,16,128]{2,1,0:T(8,128)(2,1)S(1)} %collective-permute-done.2.q_ref, bf16[2,1024,128]{2,1,0:T(8,128)(2,1)S(1)} %get-tuple-element.5.kv_own_ref, bf16[2,1024,128]{2,1,0:T(8,128)(2,1)S(1)} %collective-permute-done.1.kv_next_ref), custom_call_target="tpu_custom_call" | custom-call | flops 1073741824 | bytes 1572864 | tf_op jit(solution)/shard_map/near1/pallas_call | solution.py:116
  24.0 0.7 %collective-permute-start.4 = (bf16[1056,128]{1,0:T(8,128)(2,1)S(1)}, bf16[1056,128]{1,0:T(8,128)(2,1)S(1)}, u32[]{:S(2)}, u32[]{:S(2)}) collective-permute-start(bf16[1056,128]{1,0:T(8,128)(2,1)S(1)} %near1.1), channel_id=1, source_target_pairs={{8,16},{16,8},{9,17},{17,9},{10,18},{18,10},{11,19},{19,11},{12,20... | collective-permute-start | bytes 811016 | tf_op jit(solution)/shard_map/ppermute | solution.py:205
  24.7 6.9 %collective-permute-done.5.q_ref = bf16[128,16,128]{2,1,0:T(8,128)(2,1)S(1)} collective-permute-done((bf16[128,16,128]{2,1,0:T(8,128)(2,1)S(1)}, bf16[128,16,128]{2,1,0:T(8,128)(2,1)S(1)}, u32[]{:S(2)}, u32[]{:S(2)}) %collective-permute-start.5) | collective-permute-done | bytes 524320 | tf_op jit(solution)/shard_map/ppermute | solution.py:200
  31.6 3.2 %far1.1 = bf16[1056,128]{1,0:T(8,128)(2,1)S(1)} custom-call(s32[1]{0:T(128)S(6)} %copy.9.length_ref, bf16[128,16,128]{2,1,0:T(8,128)(2,1)S(1)} %collective-permute-done.5.q_ref, bf16[2,1024,128]{2,1,0:T(8,128)(2,1)S(1)} %get-tuple-element.5.kv_own_ref, bf16[2,1024,128]{2,1,0:T(8,128)(2,1)S(1)} %collective-permute-done.1.kv_next_ref), custom_call_target="tpu_custom_call" | custom-call | flops 1073741824 | bytes 1572864 | tf_op jit(solution)/shard_map/far1/pallas_call | solution.py:116
  34.8 1.3 %collective-permute-start.7 = (bf16[1056,128]{1,0:T(8,128)(2,1)S(1)}, bf16[1056,128]{1,0:T(8,128)(2,1)S(1)}, u32[]{:S(2)}, u32[]{:S(2)}) collective-permute-start(bf16[1056,128]{1,0:T(8,128)(2,1)S(1)} %far1.1), channel_id=1, source_target_pairs={{16,0},{8,24},{17,1},{9,25},{18,2},{10,26},{19,3},{11,27},{20,4},{... | collective-permute-start | bytes 811016 | tf_op jit(solution)/shard_map/ppermute | solution.py:207
  36.1 5.3 %collective-permute-done.kv_next_ref = bf16[2,1024,128]{2,1,0:T(8,128)(2,1)S(1)} collective-permute-done((bf16[2,1024,128]{2,1,0:T(8,128)(2,1)S(1)}, bf16[2,1024,128]{2,1,0:T(8,128)(2,1)S(1)}, u32[]{:S(2)}, u32[]{:S(2)}) %collective-permute-start) | collective-permute-done | bytes 524320 | tf_op jit(solution)/shard_map/ppermute | solution.py:199
  41.5 3.2 %near0.1 = bf16[1056,128]{1,0:T(8,128)(2,1)S(1)} custom-call(s32[1]{0:T(128)S(6)} %copy.9.length_ref, bf16[128,16,128]{2,1,0:T(8,128)(2,1)S(1)} %collective-permute-done.2.q_ref, bf16[2,1024,128]{2,1,0:T(8,128)(2,1)S(1)} %get-tuple-element.6.kv_own_ref, bf16[2,1024,128]{2,1,0:T(8,128)(2,1)S(1)} %collective-permute-done.kv_next_ref), custom_call_target="tpu_custom_call" | custom-call | flops 1073741824 | bytes 1572864 | tf_op jit(solution)/shard_map/near0/pallas_call | solution.py:116
  44.7 0.9 %collective-permute-start.3 = (bf16[1056,128]{1,0:T(8,128)(2,1)S(1)}, bf16[1056,128]{1,0:T(8,128)(2,1)S(1)}, u32[]{:S(2)}, u32[]{:S(2)}) collective-permute-start(bf16[1056,128]{1,0:T(8,128)(2,1)S(1)} %near0.1), channel_id=1, source_target_pairs={{8,16},{16,8},{9,17},{17,9},{10,18},{18,10},{11,19},{19,11},{12,20... | collective-permute-start | bytes 811016 | tf_op jit(solution)/shard_map/ppermute | solution.py:205
  45.5 3.2 %far0.1 = bf16[1056,128]{1,0:T(8,128)(2,1)S(1)} custom-call(s32[1]{0:T(128)S(6)} %copy.9.length_ref, bf16[128,16,128]{2,1,0:T(8,128)(2,1)S(1)} %collective-permute-done.5.q_ref, bf16[2,1024,128]{2,1,0:T(8,128)(2,1)S(1)} %get-tuple-element.6.kv_own_ref, bf16[2,1024,128]{2,1,0:T(8,128)(2,1)S(1)} %collective-permute-done.kv_next_ref), custom_call_target="tpu_custom_call" | custom-call | flops 1073741824 | bytes 1572864 | tf_op jit(solution)/shard_map/far0/pallas_call | solution.py:116
  48.7 1.3 %collective-permute-start.6 = (bf16[1056,128]{1,0:T(8,128)(2,1)S(1)}, bf16[1056,128]{1,0:T(8,128)(2,1)S(1)}, u32[]{:S(2)}, u32[]{:S(2)}) collective-permute-start(bf16[1056,128]{1,0:T(8,128)(2,1)S(1)} %far0.1), channel_id=1, source_target_pairs={{16,0},{8,24},{17,1},{9,25},{18,2},{10,26},{19,3},{11,27},{20,4},{... | collective-permute-start | bytes 811016 | tf_op jit(solution)/shard_map/ppermute | solution.py:207
  50.0 3.2 %own1.1.refs_1_ = bf16[1056,128]{1,0:T(8,128)(2,1)S(1)} custom-call(s32[1]{0:T(128)S(6)} %copy.9.length_ref, bf16[128,16,128]{2,1,0:T(8,128)(2,1)S(1)} %bitcast.20, bf16[2,1024,128]{2,1,0:T(8,128)(2,1)S(1)} %get-tuple-element.5.kv_own_ref, bf16[2,1024,128]{2,1,0:T(8,128)(2,1)S(1)} %collective-permute-done.1.kv_next_ref), custom_call_target="tpu_custom_call" | custom-call | flops 1073741824 | bytes 1572864 | tf_op jit(solution)/shard_map/own1/pallas_call | solution.py:116
  53.3 3.2 %own0.1.refs_0_ = bf16[1056,128]{1,0:T(8,128)(2,1)S(1)} custom-call(s32[1]{0:T(128)S(6)} %copy.9.length_ref, bf16[128,16,128]{2,1,0:T(8,128)(2,1)S(1)} %bitcast.21, bf16[2,1024,128]{2,1,0:T(8,128)(2,1)S(1)} %get-tuple-element.6.kv_own_ref, bf16[2,1024,128]{2,1,0:T(8,128)(2,1)S(1)} %collective-permute-done.kv_next_ref), custom_call_target="tpu_custom_call" | custom-call | flops 1073741824 | bytes 1572864 | tf_op jit(solution)/shard_map/own0/pallas_call | solution.py:116
  56.5 0.0 collective-permute-done.4.refs_3_
  56.5 0.0 collective-permute-done.7.refs_5_
  56.5 0.0 collective-permute-done.3.refs_2_
  56.6 4.8 %collective-permute-done.6.refs_4_ = bf16[1056,128]{1,0:T(8,128)(2,1)S(1)} collective-permute-done((bf16[1056,128]{1,0:T(8,128)(2,1)S(1)}, bf16[1056,128]{1,0:T(8,128)(2,1)S(1)}, u32[]{:S(2)}, u32[]{:S(2)}) %collective-permute-start.6) | collective-permute-done | bytes 270368 | tf_op jit(solution)/shard_map/ppermute | solution.py:207
  61.4 1.2 %merge.1 = bf16[128,16,128]{2,1,0:T(8,128)(2,1)} custom-call(bf16[1056,128]{1,0:T(8,128)(2,1)S(1)} %own0.1.refs_0_, bf16[1056,128]{1,0:T(8,128)(2,1)S(1)} %own1.1.refs_1_, bf16[1056,128]{1,0:T(8,128)(2,1)S(1)} %collective-permute-done.3.refs_2_, bf16[1056,128]{1,0:T(8,128)(2,1)S(1)} %collective-permute-done.4.refs_3_, ...), custom_call_target="tpu_custom_call" | custom-call | tf_op jit(solution)/shard_map/merge/pallas_call | solution.py:175
Async XLA Ops:
  0.0 11.5 %collective-permute-start.2 = (bf16[128,16,128]{2,1,0:T(8,128)(2,1)}, bf16[128,16,128]{2,1,0:T(8,128)(2,1)S(1)}, u32[]{:S(2)}, u32[]{:S(2)}) collective-permute-start(bf16[128,16,128]{2,1,0:T(8,128)(2,1)} %bitcast.18), channel_id=1, source_target_pairs={{8,16},{16,8},{9,17},{17,9},{10,18},{18,10},{11,19},{19,11},{12,20... | collective-permute-start | bytes 1572872 | tf_op jit(solution)/shard_map/ppermute | solution.py:196
  2.0 6.0 %copy-start = (bf16[1,128,16,128]{3,2,1,0:T(8,128)(2,1)S(1)}, bf16[1,128,16,128]{3,2,1,0:T(8,128)(2,1)}, u32[]{:S(2)}) copy-start(bf16[1,128,16,128]{3,2,1,0:T(8,128)(2,1)} %param.4) | copy-start | bytes 1572868
  2.1 18.7 %collective-permute-start.1 = (bf16[2,1024,128]{2,1,0:T(8,128)(2,1)S(1)}, bf16[2,1024,128]{2,1,0:T(8,128)(2,1)S(1)}, u32[]{:S(2)}, u32[]{:S(2)}) collective-permute-start(bf16[2,1024,128]{2,1,0:T(8,128)(2,1)S(1)} %get-tuple-element.5.kv_own_ref), channel_id=1, source_target_pairs={{0,8},{8,0},{16,24},{24,16},{1,9},{9,1},{17,25},{25,17},{2,10},{10... | collective-permute-start | bytes 1572872 | tf_op jit(solution)/shard_map/ppermute | solution.py:201
  8.1 23.6 %collective-permute-start.5 = (bf16[128,16,128]{2,1,0:T(8,128)(2,1)S(1)}, bf16[128,16,128]{2,1,0:T(8,128)(2,1)S(1)}, u32[]{:S(2)}, u32[]{:S(2)}) collective-permute-start(bf16[128,16,128]{2,1,0:T(8,128)(2,1)S(1)} %bitcast.19), channel_id=1, source_target_pairs={{0,16},{24,8},{1,17},{25,9},{2,18},{26,10},{3,19},{27,11},{4,20},{... | collective-permute-start | bytes 1572872 | tf_op jit(solution)/shard_map/ppermute | solution.py:200
  10.7 30.7 %collective-permute-start = (bf16[2,1024,128]{2,1,0:T(8,128)(2,1)S(1)}, bf16[2,1024,128]{2,1,0:T(8,128)(2,1)S(1)}, u32[]{:S(2)}, u32[]{:S(2)}) collective-permute-start(bf16[2,1024,128]{2,1,0:T(8,128)(2,1)S(1)} %get-tuple-element.6.kv_own_ref), channel_id=1, source_target_pairs={{0,8},{8,0},{16,24},{24,16},{1,9},{9,1},{17,25},{25,17},{2,10},{10... | collective-permute-start | bytes 1572872 | tf_op jit(solution)/shard_map/ppermute | solution.py:199
  24.0 32.5 %collective-permute-start.4 = (bf16[1056,128]{1,0:T(8,128)(2,1)S(1)}, bf16[1056,128]{1,0:T(8,128)(2,1)S(1)}, u32[]{:S(2)}, u32[]{:S(2)}) collective-permute-start(bf16[1056,128]{1,0:T(8,128)(2,1)S(1)} %near1.1), channel_id=1, source_target_pairs={{8,16},{16,8},{9,17},{17,9},{10,18},{18,10},{11,19},{19,11},{12,20... | collective-permute-start | bytes 811016 | tf_op jit(solution)/shard_map/ppermute | solution.py:205
  34.8 21.7 %collective-permute-start.7 = (bf16[1056,128]{1,0:T(8,128)(2,1)S(1)}, bf16[1056,128]{1,0:T(8,128)(2,1)S(1)}, u32[]{:S(2)}, u32[]{:S(2)}) collective-permute-start(bf16[1056,128]{1,0:T(8,128)(2,1)S(1)} %far1.1), channel_id=1, source_target_pairs={{16,0},{8,24},{17,1},{9,25},{18,2},{10,26},{19,3},{11,27},{20,4},{... | collective-permute-start | bytes 811016 | tf_op jit(solution)/shard_map/ppermute | solution.py:207
  44.7 11.9 %collective-permute-start.3 = (bf16[1056,128]{1,0:T(8,128)(2,1)S(1)}, bf16[1056,128]{1,0:T(8,128)(2,1)S(1)}, u32[]{:S(2)}, u32[]{:S(2)}) collective-permute-start(bf16[1056,128]{1,0:T(8,128)(2,1)S(1)} %near0.1), channel_id=1, source_target_pairs={{8,16},{16,8},{9,17},{17,9},{10,18},{18,10},{11,19},{19,11},{12,20... | collective-permute-start | bytes 811016 | tf_op jit(solution)/shard_map/ppermute | solution.py:205
  48.7 12.6 %collective-permute-start.6 = (bf16[1056,128]{1,0:T(8,128)(2,1)S(1)}, bf16[1056,128]{1,0:T(8,128)(2,1)S(1)}, u32[]{:S(2)}, u32[]{:S(2)}) collective-permute-start(bf16[1056,128]{1,0:T(8,128)(2,1)S(1)} %far0.1), channel_id=1, source_target_pairs={{16,0},{8,24},{17,1},{9,25},{18,2},{10,26},{19,3},{11,27},{20,4},{... | collective-permute-start | bytes 811016 | tf_op jit(solution)/shard_map/ppermute | solution.py:207
